TPU v7x, 32 devices: a whole 2x2x4 slice. The times are simulated.
32 devices in a mesh: groups: 2 (over y), blk: 4 (over z), desc: 2 (over x), half: 2 (over core).
Axes of the slice: x: 2, y: 2, z: 4, core: 2. Of those that a mesh axis runs over, the one named last changes fastest.
Arguments:
- descriptors: bfloat16 [8, 2048, 128], P(('groups', 'blk'), ('desc', 'half')), parts along dimension 0, may hold values from -0.5 to 0.5
Outputs:
- best_dist: float32 [3, 8, 2048], P(None, ('groups', 'blk'), 'desc'), parts along dimension 1
- second_dist: float32 [3, 8, 2048], P(None, ('groups', 'blk'), 'desc'), parts along dimension 1
There are 2 independent parts, one for each index of `groups`. A program takes and returns all parts, laid end to end along the dimension named above; each array names one. Nothing has to cross between parts.
All inputs are finite; a program needn't handle non-finite values.
Results may differ from a plain program's by a relative error of at most 0.0003.
Values may be sent and summed in bfloat16 or wider, within the bound.
A program may use at most 64 MiB of HBM per device.

v0:
```python
import jax
import jax.numpy as jnp
from jax import lax
from jax.sharding import PartitionSpec as P


def from_behind(block, axis, distance):
    devices = range(lax.axis_size(axis))
    route = [((i - distance) % len(devices), i) for i in devices]
    return lax.ppermute(block, axis, route)


def joined(value, axis, join):
    pieces = jax.tree.map(lambda part: lax.all_gather(part, axis), value)
    head = jax.tree.map(lambda part: part[0], pieces)
    tail = jax.tree.map(lambda part: part[1:], pieces)
    total, _ = lax.scan(lambda total, section: (join(total, section), None), head, tail)
    return total


def combine(one_side, other_side):
    lowest = jnp.minimum(one_side[0], other_side[0])
    second = jnp.minimum(
        jnp.maximum(one_side[0], other_side[0]), jnp.minimum(one_side[1], other_side[1])
    )
    return (lowest, second)


def fold_lanes(lowest, second):
    while lowest.shape[1] > 1:
        middle = lowest.shape[1] // 2
        lowest, second = combine(
            (lowest[:, :middle], second[:, :middle]), (lowest[:, middle:], second[:, middle:])
        )
    return (lowest[:, 0], second[:, 0])


def squared_norms(image_rows):
    widened = image_rows.astype(jnp.float32)
    return jnp.sum(widened * widened, axis=1)


def pair_best(queries, query_norms, candidates, cand_norms):
    total_rows = candidates.shape[0]
    column_count = min(256, total_rows)
    lane_width = min(128, column_count)
    slice_count = column_count // lane_width
    pieces = candidates.reshape(total_rows // column_count, column_count, candidates.shape[1])
    norm_pieces = cand_norms.reshape(total_rows // column_count, column_count)

    def pair_visit(running, slab):
        piece, piece_norms = slab
        products = lax.dot_general(
            queries, piece, (((1,), (1,)), ((), ())), preferred_element_type=jnp.float32
        )
        partial_value = piece_norms[None, :] - 2.0 * products
        lowest, second = running
        for number in range(slice_count):
            values = partial_value[:, number * lane_width : (number + 1) * lane_width]
            second = jnp.minimum(second, jnp.maximum(lowest, values))
            lowest = jnp.minimum(lowest, values)
        return ((lowest, second), None)

    initial = jnp.full((queries.shape[0], lane_width), jnp.inf, jnp.float32)
    (lowest, second), unused = lax.scan(pair_visit, (initial, initial), (pieces, norm_pieces))
    lowest, second = fold_lanes(lowest, second)
    return (query_norms + lowest, query_norms + second)


def one_way(block_rows, measure, ahead):

    def one_visit(current, unused):
        arrived = ahead(current)
        return (arrived, measure(arrived))

    unused_last, results = lax.scan(one_visit, block_rows, None, length=lax.axis_size("blk") - 1)
    return results


def per_device(descriptors):
    queries = lax.all_gather(descriptors, "half", axis=1, tiled=True)[0]
    candidates = lax.all_gather(descriptors, "desc", axis=1, tiled=True)[0]
    query_norms = squared_norms(queries)

    def measure_cand(arrived):
        return pair_best(queries, query_norms, arrived, squared_norms(arrived))

    def cand_step(current):
        return from_behind(current, "blk", 1)

    results = one_way(candidates, measure_cand, cand_step)
    best_dist, second_dist = joined(results, "half", combine)
    return (best_dist[:, None, :], second_dist[:, None, :])


def solution(mesh):
    in_specs = (P(("groups", "blk"), ("desc", "half"), None),)
    out_specs = (P(None, ("groups", "blk"), "desc"), P(None, ("groups", "blk"), "desc"))
    return jax.shard_map(
        per_device, mesh=mesh, in_specs=in_specs, out_specs=out_specs, check_vma=False
    )
```

profile of v0, /device:TPU:0, one launch (start us, length us, event | category | flops | bytes accessed | tf_op | source)
XLA Modules:
  0.0 54.5 jit_solution(8303374744048769653)
XLA Ops:
  0.6 2.3 %all_gather.19 = bf16[1,1024,128]{2,1,0:T(8,128)(2,1)S(1)} all-gather(bf16[1,512,128]{2,1,0:T(8,128)(2,1)} %param.5), channel_id=1, replica_groups=mesh['groups'=2,'blk'=4,'desc'=2,'half'=2] {'half'}, dimensions={1}, use_global_device_ids=true | all-gather | bytes 393216 | tf_op jit(solution)/shard_map/all_gather | solution.py:81
  3.0 0.2 multiply_reduce_fusion.1
  3.2 0.7 %copy-done = bf16[1,512,128]{2,1,0:T(8,128)(2,1)S(1)} copy-done((bf16[1,512,128]{2,1,0:T(8,128)(2,1)S(1)}, bf16[1,512,128]{2,1,0:T(8,128)(2,1)}, u32[]{:S(2)}) %copy-start) | copy-done | bytes 131096
  3.9 7.3 %all_gather.18 = bf16[1,1024,128]{2,1,0:T(8,128)(2,1)S(1)} all-gather(bf16[1,512,128]{2,1,0:T(8,128)(2,1)S(1)} %copy-done), channel_id=1, replica_groups=mesh['groups'=2,'blk'=4,'desc'=2,'half'=2] {'desc'}, dimensions={1}, use_global_device_ids=true | all-gather | bytes 393216 | tf_op jit(solution)/shard_map/all_gather | solution.py:82
  11.2 38.4 %while.33 = (s32[]{:T(128)}, bf16[1024,128]{1,0:T(8,128)(2,1)S(1)}, f32[3,1024]{1,0:T(4,128)S(1)}, f32[3,1024]{1,0:T(4,128)S(1)}, f32[1024]{0:T(1024)S(1)}, /*in...) while((s32[]{:T(128)}, bf16[1024,128]{1,0:T(8,128)(2,1)S(1)}, ...), condition=%wide.region_5.6_spmd, body=%wide.region_1.5_spmd.sunk | while | flops 69596160 | bytes 9514316 | solution.py:76
  11.2 1.8 %collective-permute-start = (bf16[1024,128]{1,0:T(8,128)(2,1)S(1)}, bf16[1024,128]{1,0:T(8,128)(2,1)S(1)}, u32[]{:S(2)}, u32[]{:S(2)}) collective-permute-start(bf16[1024,128]{1,0:T(8,128)(2,1)S(1)} %get-tuple-element.308), channel_id=1, source_target_pairs={{12,0},{0,4},{4,8},{8,12},{13,1},{1,5},{5,9},{9,13},{14,2},{2,6},{... | collective-permute-start | bytes 786440 | tf_op jit(solution)/shard_map/while/body/eval_jaxpr/ppermute | solution.py:10
  13.0 7.8 %collective-permute-done = bf16[1024,128]{1,0:T(8,128)(2,1)S(1)} collective-permute-done((bf16[1024,128]{1,0:T(8,128)(2,1)S(1)}, bf16[1024,128]{1,0:T(8,128)(2,1)S(1)}, u32[]{:S(2)}, u32[]{:S(2)}) %collective-permute-start) | collective-permute-done | bytes 262176 | tf_op jit(solution)/shard_map/while/body/eval_jaxpr/ppermute | solution.py:10
  20.8 0.2 multiply_reduce_fusion.3
  21.0 3.3 %while.34 = (s32[]{:T(128)}, f32[1024,128]{0,1:T(8,128)S(1)}, f32[1024,128]{0,1:T(8,128)S(1)}, f32[4,256]{1,0:T(4,128)S(1)}, bf16[4,256,128]{2,1,0:T(8,128)(2,1)...) while((s32[]{:T(128)}, f32[1024,128]{0,1:T(8,128)S(1)}, ...), condition=%wide.region_4.4_spmd.clone, body=%wide.region_3.3_spmd.clone.sunk | while | flops 68681728 | bytes 4525159 | solution.py:65
  21.0 0.3 fusion.31
  21.3 0.5 fusion.32
  21.8 0.3 fusion.31
  22.2 0.5 fusion.32
  22.7 0.3 fusion.31
  23.0 0.5 fusion.32
  23.5 0.3 fusion.31
  23.8 0.5 fusion.32
  24.5 0.1 dynamic_update_slice.10
  24.8 8.7 %collective-permute-done = bf16[1024,128]{1,0:T(8,128)(2,1)S(1)} collective-permute-done((bf16[1024,128]{1,0:T(8,128)(2,1)S(1)}, bf16[1024,128]{1,0:T(8,128)(2,1)S(1)}, u32[]{:S(2)}, u32[]{:S(2)}) %collective-permute-start) | collective-permute-done | bytes 262176 | tf_op jit(solution)/shard_map/while/body/eval_jaxpr/ppermute | solution.py:10
  33.5 0.2 multiply_reduce_fusion.3
  33.7 3.3 %while.34 = (s32[]{:T(128)}, f32[1024,128]{0,1:T(8,128)S(1)}, f32[1024,128]{0,1:T(8,128)S(1)}, f32[4,256]{1,0:T(4,128)S(1)}, bf16[4,256,128]{2,1,0:T(8,128)(2,1)...) while((s32[]{:T(128)}, f32[1024,128]{0,1:T(8,128)S(1)}, ...), condition=%wide.region_4.4_spmd.clone, body=%wide.region_3.3_spmd.clone.sunk | while | flops 68681728 | bytes 4525159 | solution.py:65
  33.7 0.3 fusion.31
  34.0 0.5 fusion.32
  34.5 0.3 fusion.31
  34.9 0.5 fusion.32
  35.4 0.3 fusion.31
  35.7 0.5 fusion.32
  36.2 0.3 fusion.31
  36.5 0.5 fusion.32
  37.2 0.1 dynamic_update_slice.10
  37.3 0.1 dynamic_update_slice.9
  37.5 8.1 %collective-permute-done = bf16[1024,128]{1,0:T(8,128)(2,1)S(1)} collective-permute-done((bf16[1024,128]{1,0:T(8,128)(2,1)S(1)}, bf16[1024,128]{1,0:T(8,128)(2,1)S(1)}, u32[]{:S(2)}, u32[]{:S(2)}) %collective-permute-start) | collective-permute-done | bytes 262176 | tf_op jit(solution)/shard_map/while/body/eval_jaxpr/ppermute | solution.py:10
  45.6 0.2 multiply_reduce_fusion.3
  45.9 3.3 %while.34 = (s32[]{:T(128)}, f32[1024,128]{0,1:T(8,128)S(1)}, f32[1024,128]{0,1:T(8,128)S(1)}, f32[4,256]{1,0:T(4,128)S(1)}, bf16[4,256,128]{2,1,0:T(8,128)(2,1)...) while((s32[]{:T(128)}, f32[1024,128]{0,1:T(8,128)S(1)}, ...), condition=%wide.region_4.4_spmd.clone, body=%wide.region_3.3_spmd.clone.sunk | while | flops 68681728 | bytes 4525159 | solution.py:65
  45.9 0.3 fusion.31
  46.2 0.5 fusion.32
  46.7 0.3 fusion.31
  47.0 0.5 fusion.32
  47.5 0.3 fusion.31
  47.8 0.5 fusion.32
  48.3 0.3 fusion.31
  48.7 0.5 fusion.32
  49.4 0.1 dynamic_update_slice.10
  49.4 0.1 dynamic_update_slice.9
  49.6 1.8 %all-gather.2 = f32[2,3,1024]{2,1,0:T(4,128)S(1)} all-gather(f32[1,3,1024]{2,1,0:T(4,128)S(1)} %bitcast.42), channel_id=2, replica_groups=mesh['groups'=2,'blk'=4,'desc'=2,'half'=2] {'half'}, dimensions={0}, use_global_device_ids=true | all-gather | bytes 36864 | tf_op jit(solution)/shard_map/all_gather | solution.py:14
  51.4 1.8 %all-gather.3 = f32[2,3,1024]{2,1,0:T(4,128)S(1)} all-gather(f32[1,3,1024]{2,1,0:T(4,128)S(1)} %bitcast.43), channel_id=3, replica_groups=mesh['groups'=2,'blk'=4,'desc'=2,'half'=2] {'half'}, dimensions={0}, use_global_device_ids=true | all-gather | bytes 36864 | tf_op jit(solution)/shard_map/all_gather | solution.py:14
  53.2 0.6 %copy.3 = f32[3,1,1024]{2,1,0:T(1,128)} copy(f32[3,1,1024]{2,0,1:T(4,128)S(1)} %get-tuple-element.149) | data formatting | bytes 24576
  53.8 0.6 %copy.4 = f32[3,1,1024]{2,1,0:T(1,128)} copy(f32[3,1,1024]{2,0,1:T(4,128)S(1)} %get-tuple-element.148) | data formatting | bytes 24576
  (52 shorter events, 0.9 us)
Async XLA Ops:
  3.0 0.9 %copy-start = (bf16[1,512,128]{2,1,0:T(8,128)(2,1)S(1)}, bf16[1,512,128]{2,1,0:T(8,128)(2,1)}, u32[]{:S(2)}) copy-start(bf16[1,512,128]{2,1,0:T(8,128)(2,1)} %param.5) | copy-start | bytes 393220
  11.2 9.6 %collective-permute-start = (bf16[1024,128]{1,0:T(8,128)(2,1)S(1)}, bf16[1024,128]{1,0:T(8,128)(2,1)S(1)}, u32[]{:S(2)}, u32[]{:S(2)}) collective-permute-start(bf16[1024,128]{1,0:T(8,128)(2,1)S(1)} %get-tuple-element.308), channel_id=1, source_target_pairs={{12,0},{0,4},{4,8},{8,12},{13,1},{1,5},{5,9},{9,13},{14,2},{2,6},{... | collective-permute-start | bytes 786440 | tf_op jit(solution)/shard_map/while/body/eval_jaxpr/ppermute | solution.py:10
  24.7 8.8 %collective-permute-start = (bf16[1024,128]{1,0:T(8,128)(2,1)S(1)}, bf16[1024,128]{1,0:T(8,128)(2,1)S(1)}, u32[]{:S(2)}, u32[]{:S(2)}) collective-permute-start(bf16[1024,128]{1,0:T(8,128)(2,1)S(1)} %get-tuple-element.308), channel_id=1, source_target_pairs={{12,0},{0,4},{4,8},{8,12},{13,1},{1,5},{5,9},{9,13},{14,2},{2,6},{... | collective-permute-start | bytes 786440 | tf_op jit(solution)/shard_map/while/body/eval_jaxpr/ppermute | solution.py:10
  37.4 8.2 %collective-permute-start = (bf16[1024,128]{1,0:T(8,128)(2,1)S(1)}, bf16[1024,128]{1,0:T(8,128)(2,1)S(1)}, u32[]{:S(2)}, u32[]{:S(2)}) collective-permute-start(bf16[1024,128]{1,0:T(8,128)(2,1)S(1)} %get-tuple-element.308), channel_id=1, source_target_pairs={{12,0},{0,4},{4,8},{8,12},{13,1},{1,5},{5,9},{9,13},{14,2},{2,6},{... | collective-permute-start | bytes 786440 | tf_op jit(solution)/shard_map/while/body/eval_jaxpr/ppermute | solution.py:10
where the time goes:
time: 54.6 us; the launch traced here: 54.5 us
  waiting for transfers between devices  24.6 us (45%)
  blocking collectives  13.3 us (24%)
  other arithmetic  7.04 us (13%)
  matrix products  3.63 us (7%)
  local copies, waits for them, and re-layouts  2.53 us (5%)
  starting transfers between devices  1.95 us (4%)
  loops' own time  0.79 us (1%)
  between operations  0.65 us (1%)
    ppermute x3, waiting for transfers between devices, from_behind(): return lax.ppermute(block, axis, route)  24.6 us
    all_gather x1, blocking collectives, per_device(): candidates = lax.all_gather(descriptors, 'desc', axis=1, tiled=True)[0]  7.29 us
    min x12, other arithmetic, pair_visit(): second = jnp.minimum(second, jnp.maximum(lowest, values))  5.65 us
    all_gather x2, blocking collectives, joined(): pieces = jax.tree.map(lambda part: lax.all_gather(part, axis), value)  3.65 us
    dot_general x12, matrix products, pair_visit(): lax.dot_general(queries, piece, (((1,), (1,)), ((), ())), preferred_eleme...  3.63 us
    all_gather x1, blocking collectives, per_device(): queries = lax.all_gather(descriptors, 'half', axis=1, tiled=True)[0]  2.33 us
    ppermute x3, starting transfers between devices, from_behind(): return lax.ppermute(block, axis, route)  1.95 us
    unnamed x4, local copies, waits for them, and re-layouts  1.91 us
  transfers between devices with their start and end apart: 3, of which 3 were waited for; matrix products, arithmetic and copies ran while one was open for 0% of the time, Pallas kernels for 0%

commit v1 on v0

v1 whole, which is shorter than its diff:
```python
import functools

import jax
import jax.numpy as jnp
from jax import lax
from jax.experimental import pallas as pl
from jax.experimental.pallas import tpu as pltpu
from jax.sharding import PartitionSpec as P

MESH = pl.DeviceIdType.MESH


def combine(lo_a, se_a, lo_b, se_b):
    return (
        jnp.minimum(lo_a, lo_b),
        jnp.minimum(jnp.maximum(lo_a, lo_b), jnp.minimum(se_a, se_b)),
    )


def nt_dot(a, b):
    return lax.dot_general(a, b, (((1,), (1,)), ((), ())), preferred_element_type=jnp.float32)


def kernel(
    n, D, H, CH, x_ref, best_ref, second_ref,
    buf, q, qn, low, sec, mine, inbox,
    z_send, z_recv, q_send, q_recv, p_send, p_recv,
):
    R = x_ref.shape[0]
    CR = R // CH
    share = H * R
    Q = D * share
    TQ = min(256, share)
    i = lax.axis_index("blk")
    d = lax.axis_index("desc")
    h = lax.axis_index("half")
    others = [(dd, hh) for dd in range(D) for hh in range(H) if (dd, hh) != (0, 0)]

    def peer(dd, hh):
        return {"desc": lax.rem(d + dd, D), "half": lax.rem(h + hh, H)}

    def rows_of(d_at, h_at):
        return pl.ds(pl.multiple_of((d_at * H + h_at) * R, R), R)

    def chunk(c):
        return pl.ds(pl.multiple_of(c * CR, CR), CR)

    def inside(j):
        return (j >= 0) & (j < n)

    barrier = pltpu.get_barrier_semaphore()
    for step in (1, -1):
        @pl.when(inside(i + step))
        def _():
            pl.semaphore_signal(barrier, inc=1, device_id={"blk": i + step}, device_id_type=MESH)
    for dd, hh in others:
        pl.semaphore_signal(barrier, inc=1, device_id=peer(dd, hh), device_id_type=MESH)
    links = jnp.where(inside(i + 1), 1, 0) + jnp.where(inside(i - 1), 1, 0)
    pl.semaphore_wait(barrier, len(others) + links)

    def own_copy(way, c):
        step = 1 - 2 * way
        return pltpu.make_async_remote_copy(
            src_ref=x_ref.at[chunk(c)], dst_ref=buf.at[i, chunk(c)],
            send_sem=z_send.at[way, i, c], recv_sem=z_recv.at[i, c],
            device_id={"blk": i + step}, device_id_type=MESH,
        )

    def relay_copy(way, j, c):
        step = 1 - 2 * way
        return pltpu.make_async_remote_copy(
            src_ref=buf.at[j, chunk(c)], dst_ref=buf.at[j, chunk(c)],
            send_sem=z_send.at[way, j, c], recv_sem=z_recv.at[j, c],
            device_id={"blk": i + step}, device_id_type=MESH,
        )

    for c in range(CH):
        for way in (0, 1):
            @pl.when(inside(i + 1 - 2 * way))
            def _():
                own_copy(way, c).start()

    mine_rows = rows_of(d, h)

    def query_copy(dd, hh):
        return pltpu.make_async_remote_copy(
            src_ref=x_ref, dst_ref=q.at[mine_rows],
            send_sem=q_send.at[dd * H + hh], recv_sem=q_recv.at[dd * H + hh],
            device_id=peer(dd, hh), device_id_type=MESH,
        )

    def query_relay(dd, hh):
        src_rows = rows_of(lax.rem(d + D - dd, D), h)
        return pltpu.make_async_remote_copy(
            src_ref=q.at[src_rows], dst_ref=q.at[src_rows],
            send_sem=q_send.at[dd * H + hh], recv_sem=q_recv.at[dd * H + hh],
            device_id=peer(0, hh), device_id_type=MESH,
        )

    for dd in range(1, D):
        query_copy(dd, 0).start()
    for hh in range(1, H):
        query_copy(0, hh).start()

    q[mine_rows, :] = x_ref[...]
    low[...] = jnp.full(low.shape, jnp.inf, jnp.float32)
    sec[...] = jnp.full(sec.shape, jnp.inf, jnp.float32)

    units = (n - 1) * CH * 2
    ahead = CH * 2

    def place(u):
        way = lax.rem(u, 2)
        c = lax.rem(lax.div(u, 2), CH)
        s = lax.div(u, 2 * CH) + 1
        j = jnp.where(way == 0, i - s, i + s)
        return way, c, s, j

    def relay(u):
        way, c, s, j = place(u)

        @pl.when(inside(j) & inside(i + 1 - 2 * way) & (u < units))
        def _():
            copy = relay_copy(way, j, c)
            copy.wait_recv()
            copy.start()

    def relays(u, carry):
        relay(u)
        return carry

    lax.fori_loop(0, ahead, relays, 0)

    for dd in range(1, D):
        query_copy(dd, 0).wait_recv()
        for hh in range(1, H):
            query_relay(dd, hh).start()
    for dd in range(D):
        for hh in range(1, H):
            query_copy(dd, hh).wait_recv()

    ones = jnp.ones((8, q.shape[1]), jnp.bfloat16)
    for t in range(D):
        wide = q[t * share : (t + 1) * share, :].astype(jnp.float32)
        square = wide * wide
        head = square.astype(jnp.bfloat16)
        tail = (square - head.astype(jnp.float32)).astype(jnp.bfloat16)
        qn[t] = nt_dot(ones, head) + nt_dot(ones, tail)

    def result_copy(k, dd, hh):
        return pltpu.make_async_remote_copy(
            src_ref=mine.at[k, lax.rem(d + dd, D)], dst_ref=inbox.at[k, dd * H + hh],
            send_sem=p_send.at[k, dd * H + hh], recv_sem=p_recv.at[k, dd * H + hh],
            device_id=peer(dd, hh), device_id_type=MESH,
        )

    def work(u, carry):
        relay(u + ahead)
        way, c, s, j = place(u)

        @pl.when(inside(j))
        def _():
            @pl.when(jnp.logical_not(inside(i + 1 - 2 * way)))
            def _():
                relay_copy(way, j, c).wait_recv()

            k = jnp.where(way == 0, s, n - s) - 1
            piece = buf[j, chunk(c), :]
            wide = piece.astype(jnp.float32)
            norms = jnp.sum(wide * wide, axis=1, keepdims=True)
            scaled = (wide * -2.0).astype(jnp.bfloat16)
            for t in range(Q // TQ):
                lanes = slice(t * TQ, (t + 1) * TQ)
                part = nt_dot(scaled, q[lanes, :]) + norms
                lo, se = low[k, :, lanes], sec[k, :, lanes]
                for r in range(CR // 8):
                    value = part[8 * r : 8 * r + 8]
                    se = jnp.minimum(se, jnp.maximum(lo, value))
                    lo = jnp.minimum(lo, value)
                low[k, :, lanes] = lo
                sec[k, :, lanes] = se

            @pl.when(c == CH - 1)
            def _():
                for t in range(D):
                    lanes = slice(t * share, (t + 1) * share)
                    lo, se = low[k, :, lanes], sec[k, :, lanes]
                    for turn in (4, 2, 1):
                        lo, se = combine(
                            lo, se, pltpu.roll(lo, turn, 0), pltpu.roll(se, turn, 0)
                        )
                    mine[k, t, 0:1, :] = lo[0:1]
                    mine[k, t, 1:2, :] = se[0:1]
                for dd, hh in reversed(others):
                    result_copy(k, dd, hh).start()

        return carry

    lax.fori_loop(0, units, work, 0)

    def finish(k, carry):
        lo, se = mine[k, d, 0:1, :], mine[k, d, 1:2, :]
        for dd, hh in others:
            result_copy(k, dd, hh).wait_recv()
            at = dd * H + hh
            lo, se = combine(lo, se, inbox[k, at, 0:1, :], inbox[k, at, 1:2, :])
        norms = qn[d, 0:1, :]
        best_ref[k] = norms + lo
        second_ref[k] = norms + se
        return carry

    lax.fori_loop(0, n - 1, finish, 0)

    def sent_results(k, carry):
        for dd, hh in others:
            result_copy(k, dd, hh).wait_send()
        return carry

    lax.fori_loop(0, n - 1, sent_results, 0)

    def sent_relays(u, carry):
        way, c, s, j = place(u)

        @pl.when(inside(j) & inside(i + 1 - 2 * way))
        def _():
            relay_copy(way, j, c).wait_send()

        return carry

    lax.fori_loop(0, units, sent_relays, 0)
    for c in range(CH):
        for way in (0, 1):
            @pl.when(inside(i + 1 - 2 * way))
            def _():
                own_copy(way, c).wait_send()
    for dd in range(1, D):
        query_copy(dd, 0).wait_send()
        for hh in range(1, H):
            query_relay(dd, hh).wait_send()
    for hh in range(1, H):
        query_copy(0, hh).wait_send()


def solution(mesh):
    n, D, H = mesh.shape["blk"], mesh.shape["desc"], mesh.shape["half"]

    def per_device(descriptors):
        block = descriptors[0]
        R, depth = block.shape
        CH = 2 if R % 32 == 0 else 1
        share = H * R
        out = jax.ShapeDtypeStruct((n - 1, 1, share), jnp.float32)
        vmem = pl.BlockSpec(memory_space=pltpu.VMEM)
        return pl.pallas_call(
            functools.partial(kernel, n, D, H, CH),
            out_shape=(out, out),
            in_specs=[vmem],
            out_specs=(vmem, vmem),
            scratch_shapes=[
                pltpu.VMEM((n, R, depth), jnp.bfloat16),
                pltpu.VMEM((D * share, depth), jnp.bfloat16),
                pltpu.VMEM((D, 8, share), jnp.float32),
                pltpu.VMEM((n - 1, 8, D * share), jnp.float32),
                pltpu.VMEM((n - 1, 8, D * share), jnp.float32),
                pltpu.VMEM((n - 1, D, 2, share), jnp.float32),
                pltpu.VMEM((n - 1, D * H, 2, share), jnp.float32),
                pltpu.SemaphoreType.DMA((2, n, CH)),
                pltpu.SemaphoreType.DMA((n, CH)),
                pltpu.SemaphoreType.DMA((D * H,)),
                pltpu.SemaphoreType.DMA((D * H,)),
                pltpu.SemaphoreType.DMA((n - 1, D * H)),
                pltpu.SemaphoreType.DMA((n - 1, D * H)),
            ],
            compiler_params=pltpu.CompilerParams(collective_id=0, has_side_effects=True),
        )(block)

    in_specs = (P(("groups", "blk"), ("desc", "half"), None),)
    out_specs = (P(None, ("groups", "blk"), "desc"), P(None, ("groups", "blk"), "desc"))
    return jax.shard_map(
        per_device, mesh=mesh, in_specs=in_specs, out_specs=out_specs, check_vma=False
    )
```

time: 54.6 us -> 24.4 us (0.45)
  waiting for transfers between devices: 24.6 us -> 0 us
  Pallas kernels: 0 us -> 21.6 us
  blocking collectives: 13.3 us -> 0 us
  other arithmetic: 7.04 us -> 0 us
  matrix products: 3.63 us -> 0 us
  starting transfers between devices: 1.95 us -> 0 us
  loops' own time: 0.79 us -> 0 us
  local copies, waits for them, and re-layouts: 2.53 us -> 1.92 us
    ppermute x3 -> x0, waiting for transfers between devices: 24.6 us -> none  [from_behind(): return lax.ppermute(block, axis, route)]
    pallas_call x0 -> x1, Pallas kernels: none -> 21.6 us  [per_device(): pl.pallas_call(functools.partial(kernel, n, D, H, CH), out_shape=(out, ou...]
    all_gather x4 -> x0, blocking collectives: 13.3 us -> none  [the longest x1 7.29 us: per_device(): candidates = lax.all_gather(descriptors, 'desc', axis=1, tiled=True)[0]]
    min x31 -> x0, other arithmetic: 6.15 us -> none  [the longest x12 5.65 us: pair_visit(): second = jnp.minimum(second, jnp.maximum(lowest, values))]
    dot_general x12 -> x0, matrix products: 3.63 us -> none  [pair_visit(): lax.dot_general(queries, piece, (((1,), (1,)), ((), ())), preferred_eleme...]
    ppermute x3 -> x0, starting transfers between devices: 1.95 us -> none  [from_behind(): return lax.ppermute(block, axis, route)]
    reduce_sum x4 -> x0, other arithmetic: 0.83 us -> none  [squared_norms(): return jnp.sum(widened * widened, axis=1)]
    another operation x4 -> x0, loops' own time: 0.79 us -> none  [the longest x3 0.43 us: pair_best(): lax.scan(pair_visit, (initial, initial), (pieces, norm_pieces))]
  transfers between devices with their start and end apart: 3 -> 0, of which waited for: 3 -> 0; matrix products, arithmetic and copies ran while one was open for 0% -> 0% of each run, Pallas kernels for 0% -> 0%
where the time goes in v1:
time: 24.4 us; the launch traced here: 24.2 us
  Pallas kernels  21.6 us (89%)
  local copies, waits for them, and re-layouts  1.92 us (8%)
  between operations  0.65 us (3%)
    pallas_call x1, Pallas kernels, per_device(): pl.pallas_call(functools.partial(kernel, n, D, H, CH), out_shape=(out, ou...  21.6 us
    unnamed x4, local copies, waits for them, and re-layouts  1.92 us

profile of v1, /device:TPU:0, one launch (start us, length us, event | category | flops | bytes accessed | tf_op | source)
XLA Modules:
  0.0 24.2 jit_solution(4642488650368246422)
XLA Ops:
  0.6 21.6 %shard_map.30 = (f32[3,1,1024]{2,1,0:T(1,128)}, f32[3,1,1024]{2,1,0:T(1,128)}) custom-call(bf16[512,128]{1,0:T(8,128)(2,1)} %bitcast.1), custom_call_target="tpu_custom_call" | custom-call | tf_op jit(solution)/shard_map/pallas_call | solution.py:254
  22.3 0.0 copy-start
  22.3 1.3 %copy.5 = f32[3,1,1024]{2,1,0:T(1,128)} copy(f32[3,1,1024]{2,1,0:T(1,128)} %get-tuple-element.4) | data formatting | bytes 24576
  23.6 0.0 copy-done
  23.6 0.6 %copy.6 = f32[3,1,1024]{2,1,0:T(1,128)} copy(f32[3,1,1024]{2,1,0:T(1,128)S(1)} %copy-done) | data formatting | bytes 24576
Async XLA Ops:
  22.3 1.3 %copy-start = (f32[3,1,1024]{2,1,0:T(1,128)S(1)}, f32[3,1,1024]{2,1,0:T(1,128)}, u32[]{:S(2)}) copy-start(f32[3,1,1024]{2,1,0:T(1,128)} %get-tuple-element.5) | copy-start | bytes 36868

commit v2 on v1

--- a/solution.py
+++ b/solution.py
@@ -22,11 +22,13 @@
 
 
 def kernel(
-    n, D, H, CH, x_ref, best_ref, second_ref,
-    buf, q, qn, low, sec, mine, inbox,
-    z_send, z_recv, q_send, q_recv, p_send, p_recv,
+    n, D, H, CH, x_hbm, best_ref, second_ref, norm_ref,
+    x_ref, buf, q, qn, low, sec, mine, inbox,
+    x_sem, z_send, z_recv, q_send, q_recv, p_send, p_recv,
 ):
-    R = x_ref.shape[0]
+    R = x_hbm.shape[0]
+    load = pltpu.make_async_copy(x_hbm, x_ref, x_sem)
+    load.start()
     CR = R // CH
     share = H * R
     Q = D * share
@@ -56,6 +58,9 @@
     for dd, hh in others:
         pl.semaphore_signal(barrier, inc=1, device_id=peer(dd, hh), device_id_type=MESH)
     links = jnp.where(inside(i + 1), 1, 0) + jnp.where(inside(i - 1), 1, 0)
+    low[...] = jnp.full(low.shape, jnp.inf, jnp.float32)
+    sec[...] = jnp.full(sec.shape, jnp.inf, jnp.float32)
+    load.wait()
     pl.semaphore_wait(barrier, len(others) + links)
 
     def own_copy(way, c):
@@ -103,8 +108,6 @@
         query_copy(0, hh).start()
 
     q[mine_rows, :] = x_ref[...]
-    low[...] = jnp.full(low.shape, jnp.inf, jnp.float32)
-    sec[...] = jnp.full(sec.shape, jnp.inf, jnp.float32)
 
     units = (n - 1) * CH * 2
     ahead = CH * 2
@@ -205,8 +208,9 @@
             at = dd * H + hh
             lo, se = combine(lo, se, inbox[k, at, 0:1, :], inbox[k, at, 1:2, :])
         norms = qn[d, 0:1, :]
-        best_ref[k] = norms + lo
-        second_ref[k] = norms + se
+        best_ref[k] = lo
+        second_ref[k] = se
+        norm_ref[...] = norms
         return carry
 
     lax.fori_loop(0, n - 1, finish, 0)
@@ -249,14 +253,15 @@
         R, depth = block.shape
         CH = 2 if R % 32 == 0 else 1
         share = H * R
-        out = jax.ShapeDtypeStruct((n - 1, 1, share), jnp.float32)
+        out = pltpu.VMEM((n - 1, 1, share), jnp.float32)
         vmem = pl.BlockSpec(memory_space=pltpu.VMEM)
-        return pl.pallas_call(
+        lo, se, norms = pl.pallas_call(
             functools.partial(kernel, n, D, H, CH),
-            out_shape=(out, out),
-            in_specs=[vmem],
-            out_specs=(vmem, vmem),
+            out_shape=(out, out, pltpu.VMEM((1, share), jnp.float32)),
+            in_specs=[pl.BlockSpec(memory_space=pltpu.HBM)],
+            out_specs=(vmem, vmem, vmem),
             scratch_shapes=[
+                pltpu.VMEM((R, depth), jnp.bfloat16),
                 pltpu.VMEM((n, R, depth), jnp.bfloat16),
                 pltpu.VMEM((D * share, depth), jnp.bfloat16),
                 pltpu.VMEM((D, 8, share), jnp.float32),
@@ -264,6 +269,7 @@
                 pltpu.VMEM((n - 1, 8, D * share), jnp.float32),
                 pltpu.VMEM((n - 1, D, 2, share), jnp.float32),
                 pltpu.VMEM((n - 1, D * H, 2, share), jnp.float32),
+                pltpu.SemaphoreType.DMA,
                 pltpu.SemaphoreType.DMA((2, n, CH)),
                 pltpu.SemaphoreType.DMA((n, CH)),
                 pltpu.SemaphoreType.DMA((D * H,)),
@@ -273,6 +279,7 @@
             ],
             compiler_params=pltpu.CompilerParams(collective_id=0, has_side_effects=True),
         )(block)
+        return norms + lo, norms + se
 
     in_specs = (P(("groups", "blk"), ("desc", "half"), None),)
     out_specs = (P(None, ("groups", "blk"), "desc"), P(None, ("groups", "blk"), "desc"))

time: 24.4 us -> 21.6 us (0.89)
  local copies, waits for them, and re-layouts: 1.92 us -> 0 us
  Pallas kernels: 21.6 us -> 20.2 us
  other arithmetic: 0 us -> 0.63 us
    unnamed x4 -> x0, local copies, waits for them, and re-layouts: 1.92 us -> none
    pallas_call x1, Pallas kernels: 21.6 us -> 20.2 us  [per_device(): pl.pallas_call(functools.partial(kernel, n, D, H, CH), out_shape=(out, ou...]
    add x0 -> x1, other arithmetic: none -> 0.63 us  [per_device(): return (norms + lo, norms + se)]
where the time goes in v2:
time: 21.6 us; the launch traced here: 21.4 us
  Pallas kernels  20.2 us (94%)
  between operations  0.64 us (3%)
  other arithmetic  0.63 us (3%)
    pallas_call x1, Pallas kernels, per_device(): pl.pallas_call(functools.partial(kernel, n, D, H, CH), out_shape=(out, ou...  20.2 us
    add x1, other arithmetic, per_device(): return (norms + lo, norms + se)  0.63 us

profile of v2, /device:TPU:0, one launch (start us, length us, event | category | flops | bytes accessed | tf_op | source)
XLA Modules:
  0.0 21.4 jit_solution(13688245230213323664)
XLA Ops:
  0.6 20.2 %shard_map.30 = (f32[3,1,1024]{2,1,0:T(1,128)S(1)}, f32[3,1,1024]{2,1,0:T(1,128)S(1)}, f32[1,1024]{1,0:T(1,128)S(1)}) custom-call(bf16[512,128]{1,0:T(8,128)(2,1)} %bitcast.3), custom_call_target="tpu_custom_call" | custom-call | tf_op jit(solution)/shard_map/pallas_call | solution.py:258
  20.8 0.6 %broadcast_add_fusion = (f32[3,1,1024]{2,1,0:T(1,128)}, f32[3,1,1024]{2,1,0:T(1,128)}) fusion(f32[3,1,1024]{2,1,0:T(1,128)S(1)} %get-tuple-element.7, f32[1024]{0:T(1024)S(1)} %bitcast.2, f32[3,1,1024]{2,1,0:T(1,128)S(1)} %get-tuple-element.6), kind=kLoop, calls=%fused_computation | loop fusion | flops 6144 | bytes 53248 | tf_op jit(solution)/shard_map/add | solution.py:282

commit v3 on v2

--- a/solution.py
+++ b/solution.py
@@ -24,7 +24,7 @@
 def kernel(
     n, D, H, CH, x_hbm, best_ref, second_ref, norm_ref,
     x_ref, buf, q, qn, low, sec, mine, inbox,
-    x_sem, z_send, z_recv, q_send, q_recv, p_send, p_recv,
+    x_sem, f_send, z_send, z_recv, q_send, q_recv, p_send, p_recv,
 ):
     R = x_hbm.shape[0]
     load = pltpu.make_async_copy(x_hbm, x_ref, x_sem)
@@ -57,7 +57,14 @@
             pl.semaphore_signal(barrier, inc=1, device_id={"blk": i + step}, device_id_type=MESH)
     for dd, hh in others:
         pl.semaphore_signal(barrier, inc=1, device_id=peer(dd, hh), device_id_type=MESH)
-    links = jnp.where(inside(i + 1), 1, 0) + jnp.where(inside(i - 1), 1, 0)
+    at_end = ((i == 0) | (i == n - 1)) & (n > 2)
+    opposite = n - 1 - i
+
+    @pl.when(at_end)
+    def _():
+        pl.semaphore_signal(barrier, inc=1, device_id={"blk": opposite}, device_id_type=MESH)
+
+    links = jnp.where(at_end, 1, 0) + jnp.where(inside(i + 1), 1, 0) + jnp.where(inside(i - 1), 1, 0)
     low[...] = jnp.full(low.shape, jnp.inf, jnp.float32)
     sec[...] = jnp.full(sec.shape, jnp.inf, jnp.float32)
     load.wait()
@@ -77,6 +84,13 @@
             src_ref=buf.at[j, chunk(c)], dst_ref=buf.at[j, chunk(c)],
             send_sem=z_send.at[way, j, c], recv_sem=z_recv.at[j, c],
             device_id={"blk": i + step}, device_id_type=MESH,
+        )
+
+    def far_copy(c):
+        return pltpu.make_async_remote_copy(
+            src_ref=x_ref.at[chunk(c)], dst_ref=buf.at[i, chunk(c)],
+            send_sem=f_send.at[c], recv_sem=z_recv.at[i, c],
+            device_id={"blk": opposite}, device_id_type=MESH,
         )
 
     for c in range(CH):
@@ -85,6 +99,11 @@
             def _():
                 own_copy(way, c).start()
 
+    @pl.when(at_end)
+    def _():
+        for c in range(CH):
+            far_copy(c).start()
+
     mine_rows = rows_of(d, h)
 
     def query_copy(dd, hh):
@@ -109,30 +128,30 @@
 
     q[mine_rows, :] = x_ref[...]
 
-    units = (n - 1) * CH * 2
-    ahead = CH * 2
-
-    def place(u):
-        way = lax.rem(u, 2)
-        c = lax.rem(lax.div(u, 2), CH)
-        s = lax.div(u, 2 * CH) + 1
-        j = jnp.where(way == 0, i - s, i + s)
-        return way, c, s, j
-
-    def relay(u):
-        way, c, s, j = place(u)
-
-        @pl.when(inside(j) & inside(i + 1 - 2 * way) & (u < units))
+    def each(steps, body):
+        def over_steps(s, carry):
+            def over_chunks(c, carry):
+                def over_ways(way, carry):
+                    body(s, c, way, i - s + 2 * s * way)
+                    return carry
+
+                return lax.fori_loop(0, 2, over_ways, carry)
+
+            return lax.fori_loop(0, CH, over_chunks, carry)
+
+        lax.fori_loop(1, 1 + steps, over_steps, 0)
+
+    def passes(way, s, j):
+        return inside(j) & inside(i + 1 - 2 * way) & (s + 1 < n - 1)
+
+    def relay(s, c, way, j):
+        @pl.when(passes(way, s, j) & (s < n))
         def _():
             copy = relay_copy(way, j, c)
             copy.wait_recv()
             copy.start()
 
-    def relays(u, carry):
-        relay(u)
-        return carry
-
-    lax.fori_loop(0, ahead, relays, 0)
+    each(1, relay)
 
     for dd in range(1, D):
         query_copy(dd, 0).wait_recv()
@@ -157,13 +176,12 @@
             device_id=peer(dd, hh), device_id_type=MESH,
         )
 
-    def work(u, carry):
-        relay(u + ahead)
-        way, c, s, j = place(u)
+    def work(s, c, way, j):
+        relay(s + 1, c, way, j - 1 + 2 * way)
 
         @pl.when(inside(j))
         def _():
-            @pl.when(jnp.logical_not(inside(i + 1 - 2 * way)))
+            @pl.when(jnp.logical_not(passes(way, s, j)))
             def _():
                 relay_copy(way, j, c).wait_recv()
 
@@ -197,9 +215,7 @@
                 for dd, hh in reversed(others):
                     result_copy(k, dd, hh).start()
 
-        return carry
-
-    lax.fori_loop(0, units, work, 0)
+    each(n - 1, work)
 
     def finish(k, carry):
         lo, se = mine[k, d, 0:1, :], mine[k, d, 1:2, :]
@@ -213,36 +229,38 @@
         norm_ref[...] = norms
         return carry
 
-    lax.fori_loop(0, n - 1, finish, 0)
-
-    def sent_results(k, carry):
-        for dd, hh in others:
-            result_copy(k, dd, hh).wait_send()
-        return carry
-
-    lax.fori_loop(0, n - 1, sent_results, 0)
-
-    def sent_relays(u, carry):
-        way, c, s, j = place(u)
-
-        @pl.when(inside(j) & inside(i + 1 - 2 * way))
+    def sent_relay(s, c, way, j):
+        @pl.when(passes(way, s, j))
         def _():
             relay_copy(way, j, c).wait_send()
 
-        return carry
-
-    lax.fori_loop(0, units, sent_relays, 0)
+    each(n - 1, sent_relay)
     for c in range(CH):
         for way in (0, 1):
             @pl.when(inside(i + 1 - 2 * way))
             def _():
                 own_copy(way, c).wait_send()
+
+    @pl.when(at_end)
+    def _():
+        for c in range(CH):
+            far_copy(c).wait_send()
+
     for dd in range(1, D):
         query_copy(dd, 0).wait_send()
         for hh in range(1, H):
             query_relay(dd, hh).wait_send()
     for hh in range(1, H):
         query_copy(0, hh).wait_send()
+
+    lax.fori_loop(0, n - 1, finish, 0)
+
+    def sent_results(k, carry):
+        for dd, hh in others:
+            result_copy(k, dd, hh).wait_send()
+        return carry
+
+    lax.fori_loop(0, n - 1, sent_results, 0)
 
 
 def solution(mesh):
@@ -270,6 +288,7 @@
                 pltpu.VMEM((n - 1, D, 2, share), jnp.float32),
                 pltpu.VMEM((n - 1, D * H, 2, share), jnp.float32),
                 pltpu.SemaphoreType.DMA,
+                pltpu.SemaphoreType.DMA((CH,)),
                 pltpu.SemaphoreType.DMA((2, n, CH)),
                 pltpu.SemaphoreType.DMA((n, CH)),
                 pltpu.SemaphoreType.DMA((D * H,)),

time: 21.6 us -> 21.4 us (level)
  Pallas kernels: 20.2 us -> 19.9 us
    pallas_call x1, Pallas kernels: 20.2 us -> 19.9 us  [per_device(): pl.pallas_call(functools.partial(kernel, n, D, H, CH), out_shape=(out, ou...]
where the time goes in v3:
time: 21.4 us; the launch traced here: 21.2 us
  Pallas kernels  19.9 us (93%)
  between operations  0.64 us (3%)
  other arithmetic  0.63 us (3%)
    pallas_call x1, Pallas kernels, per_device(): pl.pallas_call(functools.partial(kernel, n, D, H, CH), out_shape=(out, ou...  19.9 us
    add x1, other arithmetic, per_device(): return (norms + lo, norms + se)  0.63 us

profile of v3, /device:TPU:0, one launch (start us, length us, event | category | flops | bytes accessed | tf_op | source)
XLA Modules:
  0.0 21.2 jit_solution(10977022503638096271)
XLA Ops:
  0.6 19.9 %shard_map.30 = (f32[3,1,1024]{2,1,0:T(1,128)S(1)}, f32[3,1,1024]{2,1,0:T(1,128)S(1)}, f32[1,1024]{1,0:T(1,128)S(1)}) custom-call(bf16[512,128]{1,0:T(8,128)(2,1)} %bitcast.3), custom_call_target="tpu_custom_call" | custom-call | tf_op jit(solution)/shard_map/pallas_call | solution.py:276
  20.6 0.6 %broadcast_add_fusion = (f32[3,1,1024]{2,1,0:T(1,128)}, f32[3,1,1024]{2,1,0:T(1,128)}) fusion(f32[3,1,1024]{2,1,0:T(1,128)S(1)} %get-tuple-element.7, f32[1024]{0:T(1024)S(1)} %bitcast.2, f32[3,1,1024]{2,1,0:T(1,128)S(1)} %get-tuple-element.6), kind=kLoop, calls=%fused_computation | loop fusion | flops 6144 | bytes 53248 | tf_op jit(solution)/shard_map/add | solution.py:301
